TPU v7x, 64 devices: a 2x2x8 block of a 4x4x8 slice. The times are simulated.
64 devices in a mesh: stage: 4 (over x, y), data: 16 (over z, core).
Axes of the slice: x: 2, y: 2, z: 8, core: 2. Of those that a mesh axis runs over, the one named last changes fastest.
The devices are a block of a 4x4x8 slice.
Arguments:
- w_master: float32 [128, 1536, 512], P('stage', 'data'), parts along dimension 0
- momentum: float32 [128, 1536, 512], P('stage', 'data'), parts along dimension 0
- grad: bfloat16 [128, 1536, 512], P('stage', 'data'), parts along dimension 0
Outputs:
- output 1: bfloat16 [128, 1536, 512], P('stage'), parts along dimension 0
- output 2: float32 [128, 1536, 512], P('stage', 'data'), parts along dimension 0
There are 4 independent parts. A program takes and returns all parts, laid end to end along the dimension named above; each array names one.
All inputs are finite; a program needn't handle non-finite values.
Results may differ from a plain program's by a relative error of at most 0.0073494.
Values are sent between devices in bfloat16 or wider.
A program may use at most 768 MiB of HBM per device.

v0:
```python
import math
import jax
import jax.numpy as jnp
from jax import lax
from jax.sharding import PartitionSpec as P

NS_ITERS = 5
MOMENTUM = 0.95
LEARN_RATE = 0.02
WEIGHT_DECAY = 0.1
NORM_EPS = 1e-7
COEF_A = 3.4445
COEF_B = -4.7750
COEF_C = 2.0315


def newton_schulz(x_mat):
    wide = x_mat.shape[1] <= x_mat.shape[2]
    for iteration in range(NS_ITERS):
        if wide:
            gram_mat = jnp.einsum("kip,kjp->kij", x_mat, x_mat, preferred_element_type=jnp.float32)
        else:
            gram_mat = jnp.einsum("kpi,kpj->kij", x_mat, x_mat, preferred_element_type=jnp.float32)
        gram_mat = gram_mat.astype(jnp.bfloat16)
        square = jnp.einsum("kij,kjl->kil", gram_mat, gram_mat, preferred_element_type=jnp.float32)
        poly_mat = (COEF_B * gram_mat.astype(jnp.float32) + COEF_C * square).astype(jnp.bfloat16)
        if wide:
            prod_mat = jnp.einsum("kij,kjp->kip", poly_mat, x_mat, preferred_element_type=jnp.float32)
        else:
            prod_mat = jnp.einsum("kpj,kij->kpi", x_mat, poly_mat, preferred_element_type=jnp.float32)
        x_mat = (COEF_A * x_mat.astype(jnp.float32) + prod_mat).astype(jnp.bfloat16)
    return x_mat


def solution(mesh):
    group = mesh.shape["data"]
    row_spec = P("stage", "data", None)
    full_spec = P("stage", None, None)

    def local_step(w_rows, mom_rows, grad_rows):
        mat_count, rows_dev, col_count = mom_rows.shape
        own_count = mat_count // group
        rms_scale = 0.2 * math.sqrt(max(rows_dev * group, col_count))
        mom_new = MOMENTUM * mom_rows + grad_rows.astype(jnp.float32)
        sq_total = lax.psum(jnp.sum(mom_new * mom_new, axis=(1, 2)), "data")
        owned = lax.all_to_all(mom_new.astype(jnp.bfloat16), "data", 0, 1, tiled=True)
        my_index = lax.axis_index("data")
        sq_owned = lax.dynamic_slice_in_dim(sq_total, my_index * own_count, own_count)
        x_mat = (owned.astype(jnp.float32) / (jnp.sqrt(sq_owned)[:, None, None] + NORM_EPS)).astype(jnp.bfloat16)
        x_mat = newton_schulz(x_mat)
        ortho_rows = lax.all_to_all(x_mat, "data", 1, 0, tiled=True)
        w_new = w_rows - LEARN_RATE * (ortho_rows.astype(jnp.float32) * rms_scale + WEIGHT_DECAY * w_rows)
        params = lax.all_gather(w_new.astype(jnp.bfloat16), "data", axis=1, tiled=True)
        return params, mom_new

    return jax.shard_map(local_step, mesh=mesh, in_specs=(row_spec, row_spec, row_spec), out_specs=(full_spec, row_spec), check_vma=False)
```

profile of v0, /device:TPU:21, one launch (start us, length us, event | category | flops | bytes accessed | tf_op | source)
XLA Modules:
  0.0 565.1 jit_solution(11368353284989559948)
XLA Ops:
  7.2 5.0 multiply_reduce_fusion
  12.2 0.0 copy-start
  12.2 2.7 copy-done
  14.9 2.1 convert_element_type.106
  17.0 10.7 %all-to-all-start = ((bf16[32,96,512]{2,1,0:T(8,128)(2,1)}), bf16[32,96,512]{2,1,0:T(8,128)(2,1)S(1)}, u32[]{:S(2)}, u32[]{:S(2)}) async-start(bf16[32,96,512]{2,1,0:T(8,128)(2,1)} %convert_element_type.106), calls=%async_computation | async-start | bytes 6291456 | tf_op jit(solution)/shard_map/all_to_all | solution.py:46
  27.8 0.1 all-gather.2.cloned.1.call-start
  27.8 87.2 %psum.7 = f32[32]{0:T(128)S(1)} all-reduce(f32[32]{0:T(128)S(1)} %get-tuple-element.2), channel_id=1, replica_groups=mesh['stage'=4,'data'=16] {'data'}, use_global_device_ids=true, to_apply=%region_1.0 | all-reduce | flops 32 | bytes 256 | tf_op jit(solution)/shard_map/psum | solution.py:45
  115.0 0.1 sqrt_add_fusion
  115.1 0.0 all-to-all-done
  115.1 0.9 copy.12
  116.0 1.0 fusion
  117.0 2.8 convolution_convert_fusion.4
  119.8 6.3 %add_convert_fusion.4 = bf16[2,1536,512]{2,1,0:T(8,128)(2,1)} fusion(bf16[2,1536,512]{2,1,0:T(8,128)(2,1)S(1)} %fusion, bf16[2,512,512]{2,1,0:T(8,128)(2,1)} %convolution_convert_fusion.4), kind=kOutput, calls=%fused_computation.11 | convolution fusion | flops 2156396544 | bytes 7340032 | tf_op jit(solution)/shard_map/kpj,kij->kpi/dot_general | solution.py:30
  126.1 0.0 copy-start.1
  126.1 5.8 %convolution_convert_fusion.3 = bf16[2,512,512]{2,1,0:T(8,128)(2,1)} fusion(bf16[2,1536,512]{2,1,0:T(8,128)(2,1)} %add_convert_fusion.4), kind=kOutput, calls=%fused_computation.22 | convolution fusion | flops 1611137024 | bytes 4194304 | tf_op jit(solution)/shard_map/kpi,kpj->kij/dot_general | solution.py:23
  131.8 0.0 copy-done.1
  131.9 6.1 %add_convert_fusion.3 = bf16[2,1536,512]{2,1,0:T(8,128)(2,1)} fusion(bf16[2,1536,512]{2,1,0:T(8,128)(2,1)S(1)} %copy-done.1, bf16[2,512,512]{2,1,0:T(8,128)(2,1)} %convolution_convert_fusion.3), kind=kOutput, calls=%fused_computation.10 | convolution fusion | flops 2156396544 | bytes 7340032 | tf_op jit(solution)/shard_map/kpj,kij->kpi/dot_general | solution.py:30
  138.0 0.0 copy-start.2
  138.0 5.8 %convolution_convert_fusion.2 = bf16[2,512,512]{2,1,0:T(8,128)(2,1)} fusion(bf16[2,1536,512]{2,1,0:T(8,128)(2,1)} %add_convert_fusion.3), kind=kOutput, calls=%fused_computation.21 | convolution fusion | flops 1611137024 | bytes 4194304 | tf_op jit(solution)/shard_map/kpi,kpj->kij/dot_general | solution.py:23
  143.8 0.0 copy-done.2
  143.8 6.4 %add_convert_fusion.2 = bf16[2,1536,512]{2,1,0:T(8,128)(2,1)} fusion(bf16[2,1536,512]{2,1,0:T(8,128)(2,1)S(1)} %copy-done.2, bf16[2,512,512]{2,1,0:T(8,128)(2,1)} %convolution_convert_fusion.2), kind=kOutput, calls=%fused_computation.9 | convolution fusion | flops 2156396544 | bytes 7340032 | tf_op jit(solution)/shard_map/kpj,kij->kpi/dot_general | solution.py:30
  150.2 0.0 copy-start.3
  150.2 5.8 %convolution_convert_fusion.1 = bf16[2,512,512]{2,1,0:T(8,128)(2,1)} fusion(bf16[2,1536,512]{2,1,0:T(8,128)(2,1)} %add_convert_fusion.2), kind=kOutput, calls=%fused_computation.20 | convolution fusion | flops 1611137024 | bytes 4194304 | tf_op jit(solution)/shard_map/kpi,kpj->kij/dot_general | solution.py:23
  156.0 0.0 copy-done.3
  156.0 6.1 %add_convert_fusion.1 = bf16[2,1536,512]{2,1,0:T(8,128)(2,1)} fusion(bf16[2,1536,512]{2,1,0:T(8,128)(2,1)S(1)} %copy-done.3, bf16[2,512,512]{2,1,0:T(8,128)(2,1)} %convolution_convert_fusion.1), kind=kOutput, calls=%fused_computation.8 | convolution fusion | flops 2156396544 | bytes 7340032 | tf_op jit(solution)/shard_map/kpj,kij->kpi/dot_general | solution.py:30
  162.1 5.7 convolution_convert_fusion
  167.8 6.3 %add_convert_fusion = bf16[2,1536,512]{2,1,0:T(8,128)(2,1)S(1)} fusion(bf16[2,1536,512]{2,1,0:T(8,128)(2,1)} %add_convert_fusion.1, bf16[2,512,512]{2,1,0:T(8,128)(2,1)} %convolution_convert_fusion), kind=kOutput, calls=%fused_computation.7 | convolution fusion | flops 2156396544 | bytes 7340032 | tf_op jit(solution)/shard_map/kpj,kij->kpi/dot_general | solution.py:30
  174.1 12.3 %copy.18 = bf16[2,1536,512]{2,0,1:T(2,128)(2,1)S(1)} copy(bf16[2,1536,512]{2,1,0:T(8,128)(2,1)S(1)} %add_convert_fusion) | data formatting | bytes 6291456 | tf_op jit(solution)/shard_map/convert_element_type | solution.py:31
  186.4 82.2 %all_to_all.8 = bf16[2,1536,512]{2,0,1:T(2,128)(2,1)S(1)} all-to-all(bf16[2,1536,512]{2,0,1:T(2,128)(2,1)S(1)} %copy.18), channel_id=1, replica_groups=mesh['stage'=4,'data'=16] {'data'}, dimensions={1} | all-to-all | bytes 6291456 | tf_op jit(solution)/shard_map/all_to_all | solution.py:51
  268.6 0.0 slice-start
  268.6 3.3 convert_multiply_fusion
  271.9 0.0 slice-start.1
  272.0 1.2 copy.19
  273.1 0.0 slice-done
  273.2 0.4 slice-done.1
  273.5 3.5 fusion.3
  277.0 0.1 all-gather.2.cloned.1.call-update
  277.1 247.7 %all-gather.2.cloned.1.call-done = bf16[32,1536,512]{2,1,0:T(8,128)(2,1)} async-done(((bf16[32,96,512]{2,1,0:T(8,128)(2,1)}), bf16[32,1536,512]{2,1,0:T(8,128)(2,1)}) %all-gather.2.cloned.1.call-update) | async-done | bytes 50331664 | tf_op jit(solution)/shard_map/all_gather | solution.py:53
  524.8 33.4 %copy.26 = bf16[32,1536,512]{2,1,0:T(8,128)(2,1)} copy(bf16[32,1536,512]{2,1,0:T(8,128)(2,1)} %all-gather.2.cloned.1.call-done) | data formatting | bytes 100663296
  (1 shorter events, 0.0 us)
Async XLA Ops:
  12.2 2.7 copy-start
  17.0 98.1 %all-to-all-start = ((bf16[32,96,512]{2,1,0:T(8,128)(2,1)}), bf16[32,96,512]{2,1,0:T(8,128)(2,1)S(1)}, u32[]{:S(2)}, u32[]{:S(2)}) async-start(bf16[32,96,512]{2,1,0:T(8,128)(2,1)} %convert_element_type.106), calls=%async_computation | async-start | bytes 6291456 | tf_op jit(solution)/shard_map/all_to_all | solution.py:46
  27.8 497.0 %all-gather.2.cloned.1.call-start = ((), (), s32[]{:S(2)}) async-start(), calls=%async_computation.2 | async-start | bytes 53477376 | tf_op jit(solution)/shard_map/all_gather | solution.py:53
  126.1 5.8 %copy-start.1 = (bf16[2,1536,512]{2,1,0:T(8,128)(2,1)S(1)}, bf16[2,1536,512]{2,1,0:T(8,128)(2,1)}, u32[]{:S(2)}) copy-start(bf16[2,1536,512]{2,1,0:T(8,128)(2,1)} %add_convert_fusion.4) | copy-start | bytes 9437188
  138.0 5.8 %copy-start.2 = (bf16[2,1536,512]{2,1,0:T(8,128)(2,1)S(1)}, bf16[2,1536,512]{2,1,0:T(8,128)(2,1)}, u32[]{:S(2)}) copy-start(bf16[2,1536,512]{2,1,0:T(8,128)(2,1)} %add_convert_fusion.3) | copy-start | bytes 9437188
  150.2 5.8 %copy-start.3 = (bf16[2,1536,512]{2,1,0:T(8,128)(2,1)S(1)}, bf16[2,1536,512]{2,1,0:T(8,128)(2,1)}, u32[]{:S(2)}) copy-start(bf16[2,1536,512]{2,1,0:T(8,128)(2,1)} %add_convert_fusion.2) | copy-start | bytes 9437188
  268.6 4.5 slice-start
  271.9 1.6 slice-start.1
Sparse Core Ops, SparseCore 0:
  277.2 247.5 all-gather.1
where the time goes:
time: 565 us
  waiting for transfers between devices  248 us (44%)
  blocking collectives  169 us (30%)
  matrix products  57.1 us (10%)
  local copies, waits for them, and re-layouts  51 us (9%)
  other arithmetic  15 us (3%)
  between operations  14.1 us (2%)
  starting transfers between devices  10.8 us (2%)
    all_gather x1, waiting for transfers between devices, local_step(): lax.all_gather(w_new.astype(jnp.bfloat16), 'data', axis=1, tiled=True)  248 us
    psum x1, blocking collectives, local_step(): sq_total = lax.psum(jnp.sum(mom_new * mom_new, axis=(1, 2)), 'data')  87.2 us
    all_to_all x1, blocking collectives, local_step(): ortho_rows = lax.all_to_all(x_mat, 'data', 1, 0, tiled=True)  82.2 us
    unnamed x13, local copies, waits for them, and re-layouts  36.6 us
    dot_general x5, matrix products, newton_schulz(): jnp.einsum('kpj,kij->kpi', x_mat, poly_mat, preferred_element_type=jnp.fl...  31.2 us
    dot_general x5, matrix products, newton_schulz(): jnp.einsum('kpi,kpj->kij', x_mat, x_mat, preferred_element_type=jnp.float32)  25.8 us
    convert_element_type x1, local copies, waits for them, and re-layouts, newton_schulz(): x_mat = (COEF_A * x_mat.astype(jnp.float32) + prod_mat).astype(jnp.bfloat16)  12.3 us
  transfers between devices with their start and end apart: 2, of which 1 were waited for; matrix products, arithmetic and copies ran while one was open for 0% of the time, Pallas kernels for 0%

commit v1 on v0

v1 whole, which is shorter than its diff:
```python
import functools
import math
import jax
import jax.numpy as jnp
from jax import lax
from jax.experimental import pallas as pl
from jax.experimental.pallas import tpu as pltpu
from jax.sharding import PartitionSpec as P

NS_ITERS = 5
MOMENTUM = 0.95
LEARN_RATE = 0.02
WEIGHT_DECAY = 0.1
NORM_EPS = 1e-7
COEF_A = 3.4445
COEF_B = -4.7750
COEF_C = 2.0315
CORES = 2
QUADS = 4
MESH = pl.DeviceIdType.MESH
F32 = jnp.float32
BF16 = jnp.bfloat16


def hops(quad):
    return (4, 3) if quad % 2 == 0 else (3, 4)


def newton_schulz(x_ref, gram_ref, poly_ref, denom):
    blocks, rows, cols = x_ref.shape

    def scale(j, carry):
        x_ref[j] = (x_ref[j].astype(F32) / denom).astype(BF16)
        return carry

    lax.fori_loop(0, blocks, scale, 0)
    half = cols // 2
    step = blocks // 4

    def iteration(i, carry):
        x_all = x_ref[...].reshape(blocks * rows, cols)
        gram_ref[...] = lax.dot_general(
            x_all, x_all, (((0,), (0,)), ((), ())), preferred_element_type=F32
        ).astype(BF16)
        gram = gram_ref[...]
        for p in range(2):
            part = gram_ref[p * half:(p + 1) * half, :]
            square = jnp.dot(part, gram, preferred_element_type=F32)
            poly_ref[p * half:(p + 1) * half, :] = (COEF_B * part.astype(F32) + COEF_C * square).astype(BF16)
        poly = poly_ref[...]

        def rows_of(r, inner):
            x_part = x_ref[pl.ds(r * step, step)].reshape(step * rows, cols)
            prod = jnp.dot(x_part, poly, preferred_element_type=F32)
            x_ref[pl.ds(r * step, step)] = (COEF_A * x_part.astype(F32) + prod).astype(BF16).reshape(step, rows, cols)
            return inner

        for r in range(4):
            rows_of(r, 0)
        return carry

    lax.fori_loop(0, NS_ITERS, iteration, 0)


def step_kernel(group, w_hbm, mom_hbm, grad_hbm, out_hbm,
                mom_v, grad_v, w_v, mom_b, x_v, o_v, new_v, sq_out, sq_in, gram_v, poly_v,
                in_sem, w_sem, a_send, a_recv, q_send, q_recv, o_send, o_recv,
                ring_send, ring_recv, pair_send, pair_recv, own_sem):
    count, rows, cols = mom_hbm.shape
    chips = group // CORES
    quad_mats = group // QUADS
    rms = 0.2 * math.sqrt(max(rows * group, cols))
    me = lax.axis_index("data")
    chip, core = me // CORES, me % CORES
    up = lax.rem(chip + 1, chips) * CORES + core
    down = lax.rem(chip + chips - 1, chips) * CORES + core
    pair = chip * CORES + (1 - core)

    def peer(k):
        return lax.rem(me + k, group)

    def remote(src, dst, send_sem, recv_sem, to):
        return pltpu.make_async_remote_copy(src, dst, send_sem, recv_sem, device_id={"data": to}, device_id_type=MESH)

    for s in range(2):
        def load(k, carry):
            m = s * group + peer(k)
            pltpu.make_async_copy(mom_hbm.at[m], mom_v.at[m], in_sem.at[0, m]).start()
            pltpu.make_async_copy(grad_hbm.at[m], grad_v.at[m], in_sem.at[1, m]).start()
            return carry
        lax.fori_loop(0, group, load, 0)
    for s in range(2):
        pltpu.make_async_copy(w_hbm.at[pl.ds(s * group, group)], w_v.at[pl.ds(s * group, group)], w_sem.at[s]).start()

    barrier = pltpu.get_barrier_semaphore()

    def greet(k, carry):
        pl.semaphore_signal(barrier, inc=1, device_id={"data": peer(k)}, device_id_type=MESH)
        return carry
    lax.fori_loop(1, group, greet, 0)
    pl.semaphore_wait(barrier, group - 1)

    for s in range(2):
        def send(k):
            to = peer(k)
            m = s * group + to
            remote(mom_b.at[m], x_v.at[s, me], a_send.at[s], a_recv.at[s], to).start()
            remote(sq_out.at[m], sq_in.at[s, me], q_send.at[s], q_recv.at[s], to).start()

        def momentum(k, carry):
            m = s * group + peer(k)
            pltpu.make_async_copy(mom_hbm.at[m], mom_v.at[m], in_sem.at[0, m]).wait()
            pltpu.make_async_copy(grad_hbm.at[m], grad_v.at[m], in_sem.at[1, m]).wait()
            new = MOMENTUM * mom_v[m] + grad_v[m].astype(F32)
            sq = (new * new).reshape(rows // 8, 8, cols // 128, 128)
            sq_out[m] = jnp.sum(jnp.sum(sq, axis=0), axis=1)
            mom_b[m] = new.astype(BF16)

            @pl.when(k > 1)
            def _():
                send(k - 1)
            return carry
        lax.fori_loop(0, group, momentum, 0)
        x_v[s, me] = mom_b[s * group + me]
        sq_in[s, me] = sq_out[s * group + me]
        send(group - 1)

    def owned(s, carry):
        others = pl.ds(0, group - 1)
        pltpu.make_async_copy(x_v.at[s, others], x_v.at[s, others], a_recv.at[s]).wait()
        pltpu.make_async_copy(sq_in.at[s, others], sq_in.at[s, others], q_recv.at[s]).wait()
        total = jnp.sum(jnp.sum(sq_in[s], axis=0), axis=0, keepdims=True)
        denom = jnp.sqrt(jnp.sum(total, axis=1, keepdims=True)) + NORM_EPS
        newton_schulz(x_v.at[s], gram_v, poly_v, denom)
        o_v[s * group + me] = x_v[s, me]

        def back(k, inner):
            to = peer(k)
            remote(x_v.at[s, to], o_v.at[s * group + me], o_send.at[s], o_recv.at[s], to).start()
            return inner
        lax.fori_loop(1, group, back, 0)
        return carry
    lax.fori_loop(0, 2, owned, 0)

    def block(ref, s, q, src):
        return ref.at[pl.ds(s * group + q * quad_mats, quad_mats), pl.ds(pl.multiple_of(src * rows, 32), rows), :]

    def update(s):
        others = pl.ds(0, group - 1)
        pltpu.make_async_copy(o_v.at[others], o_v.at[others], o_recv.at[s]).wait()
        pltpu.make_async_copy(w_hbm.at[pl.ds(s * group, group)], w_v.at[pl.ds(s * group, group)], w_sem.at[s]).wait()

        def one(m, carry):
            w_old = w_v[m]
            new_v[m] = (w_old - LEARN_RATE * (o_v[m].astype(F32) * rms + WEIGHT_DECAY * w_old)).astype(BF16)
            return carry
        lax.fori_loop(s * group, (s + 1) * group, one, 0)
        for q in range(QUADS):
            src = new_v.at[pl.ds(s * group + q * quad_mats, quad_mats)]
            dst = block(out_hbm, s, q, me)
            remote(src, dst, ring_send.at[0], ring_recv.at[0, s, q, 0], up).start()
            remote(src, dst, ring_send.at[1], ring_recv.at[1, s, q, 0], down).start()
            remote(src, dst, pair_send.at[0], pair_recv.at[0], pair).start()
            pltpu.make_async_copy(src, dst, own_sem.at[s]).start()

    def relay(s, h):
        for q in range(QUADS):
            for way in range(2):
                if h > hops(q)[way]:
                    continue
                src = lax.rem(chip + (chips - h if way == 0 else h), chips) * CORES + core
                blk = block(out_hbm, s, q, src)
                remote(blk, blk, ring_send.at[way], ring_recv.at[way, s, q, h - 1], (up, down)[way]).wait_recv()
                if h < hops(q)[way]:
                    remote(blk, blk, ring_send.at[way], ring_recv.at[way, s, q, h], (up, down)[way]).start()
                remote(blk, blk, pair_send.at[0], pair_recv.at[0], pair).start()

    update(0)
    relay(0, 1)
    update(1)
    relay(0, 2)
    relay(1, 1)
    relay(0, 3)
    relay(1, 2)
    relay(0, 4)
    relay(1, 3)
    relay(1, 4)

    others = pl.ds(0, group - 1)
    for s in range(2):
        pltpu.make_async_copy(x_v.at[s, others], x_v.at[s, others], a_send.at[s]).wait()
        pltpu.make_async_copy(sq_in.at[s, others], sq_in.at[s, others], q_send.at[s]).wait()
        pltpu.make_async_copy(o_v.at[others], o_v.at[others], o_send.at[s]).wait()
        own = new_v.at[pl.ds(s * group, group)]
        pltpu.make_async_copy(own, own, own_sem.at[s]).wait()
    for way in range(2):
        sent = sum(hops(q)[way] for q in range(QUADS)) * quad_mats * 2
        full = out_hbm.at[pl.ds(0, sent // group)]
        pltpu.make_async_copy(full, full, ring_send.at[way]).wait()
    full = out_hbm.at[pl.ds(0, count // 2)]
    pltpu.make_async_copy(full, full, pair_send.at[0]).wait()
    pltpu.make_async_copy(full, full, pair_recv.at[0]).wait()


def run_step(group, w_rows, mom_rows, grad_rows):
    count, rows, cols = mom_rows.shape
    any_spec = pl.BlockSpec(memory_space=pltpu.HBM)
    dma = pltpu.SemaphoreType.DMA
    return pl.pallas_call(
        functools.partial(step_kernel, group),
        out_shape=jax.ShapeDtypeStruct((count, rows * group, cols), BF16),
        in_specs=[any_spec] * 3,
        out_specs=any_spec,
        scratch_shapes=[
            pltpu.VMEM((count, rows, cols), F32),
            pltpu.VMEM((count, rows, cols), BF16),
            pltpu.VMEM((count, rows, cols), F32),
            pltpu.VMEM((count, rows, cols), BF16),
            pltpu.VMEM((2, group, rows, cols), BF16),
            pltpu.VMEM((count, rows, cols), BF16),
            pltpu.VMEM((count, rows, cols), BF16),
            pltpu.VMEM((count, 8, 128), F32),
            pltpu.VMEM((2, group, 8, 128), F32),
            pltpu.VMEM((cols, cols), BF16),
            pltpu.VMEM((cols, cols), BF16),
            dma((2, count)), dma((2,)),
            dma((2,)), dma((2,)), dma((2,)), dma((2,)), dma((2,)), dma((2,)),
            dma((2,)), dma((2, 2, QUADS, 4)), dma((1,)), dma((1,)), dma((2,)),
        ],
        compiler_params=pltpu.CompilerParams(collective_id=0, has_side_effects=True, vmem_limit_bytes=60 * 1024 * 1024),
        name="muon_step",
    )(w_rows, mom_rows, grad_rows)


def solution(mesh):
    group = mesh.shape["data"]
    row_spec = P("stage", "data", None)
    full_spec = P("stage", None, None)

    def local_step(w_rows, mom_rows, grad_rows):
        mom_new = MOMENTUM * mom_rows + grad_rows.astype(F32)
        params = run_step(group, w_rows, mom_rows, grad_rows)
        return params, mom_new

    return jax.shard_map(local_step, mesh=mesh, in_specs=(row_spec, row_spec, row_spec), out_specs=(full_spec, row_spec), check_vma=False)
```

time: 565 us -> 434 us (0.77)
  Pallas kernels: 0 us -> 393 us
  waiting for transfers between devices: 248 us -> 0 us
  blocking collectives: 169 us -> 0 us
  matrix products: 57.1 us -> 0 us
  local copies, waits for them, and re-layouts: 51 us -> 33.5 us
  between operations: 14.1 us -> 0.65 us
  starting transfers between devices: 10.8 us -> 0 us
  other arithmetic: 15 us -> 6.9 us
    pallas_call x0 -> x1, Pallas kernels: none -> 393 us  [run_step(): pl.pallas_call(functools.partial(step_kernel, group), out_shape=jax.Shape...]
    all_gather x1 -> x0, waiting for transfers between devices: 248 us -> none  [local_step(): lax.all_gather(w_new.astype(jnp.bfloat16), 'data', axis=1, tiled=True)]
    psum x1 -> x0, blocking collectives: 87.2 us -> none  [local_step(): sq_total = lax.psum(jnp.sum(mom_new * mom_new, axis=(1, 2)), 'data')]
    all_to_all x1 -> x0, blocking collectives: 82.2 us -> none  [local_step(): ortho_rows = lax.all_to_all(x_mat, 'data', 1, 0, tiled=True)]
    dot_general x10 -> x0, matrix products: 57.1 us -> none  [the longest x5 31.2 us: newton_schulz(): jnp.einsum('kpj,kij->kpi', x_mat, poly_mat, preferred_element_type=jnp.fl...]
    convert_element_type x2 -> x0, local copies, waits for them, and re-layouts: 13.2 us -> none  [the longest x1 12.3 us: newton_schulz(): x_mat = (COEF_A * x_mat.astype(jnp.float32) + prod_mat).astype(jnp.bfloat16)]
    all_to_all x1 -> x0, starting transfers between devices: 10.7 us -> none  [local_step(): lax.all_to_all(mom_new.astype(jnp.bfloat16), 'data', 0, 1, tiled=True)]
    add x1, other arithmetic: 0.08 us -> 6.9 us  [local_step(): mom_new = MOMENTUM * mom_rows + grad_rows.astype(F32)]
  transfers between devices with their start and end apart: 2 -> 0, of which waited for: 1 -> 0; matrix products, arithmetic and copies ran while one was open for 0% -> 0% of each run, Pallas kernels for 0% -> 0%
where the time goes in v1:
time: 434 us
  Pallas kernels  393 us (91%)
  local copies, waits for them, and re-layouts  33.5 us (8%)
  other arithmetic  6.9 us (2%)
    pallas_call x1, Pallas kernels, run_step(): pl.pallas_call(functools.partial(step_kernel, group), out_shape=jax.Shape...  393 us
    unnamed x3, local copies, waits for them, and re-layouts  33.5 us

profile of v1, /device:TPU:21, one launch (start us, length us, event | category | flops | bytes accessed | tf_op | source)
XLA Modules:
  0.0 434.0 jit_solution(9371037963765439665)
XLA Ops:
  0.6 0.0 copy-start
  0.6 393.0 %muon_step.1 = bf16[32,1536,512]{2,1,0:T(8,128)(2,1)} custom-call(f32[32,96,512]{2,1,0:T(8,128)} %w_hbm.1, f32[32,96,512]{2,1,0:T(8,128)} %mom_hbm.1, bf16[32,96,512]{2,1,0:T(8,128)(2,1)} %grad_hbm.1), custom_call_target="tpu_custom_call" | custom-call | tf_op jit(solution)/shard_map/muon_step/pallas_call | solution.py:209
  393.7 0.0 copy-done
  393.7 6.9 %convert_add_fusion = f32[32,96,512]{2,1,0:T(8,128)} fusion(bf16[32,96,512]{2,1,0:T(8,128)(2,1)S(1)} %copy-done, f32[32,96,512]{2,1,0:T(8,128)} %mom_hbm.1), kind=kLoop, calls=%fused_computation | loop fusion | flops 4718592 | bytes 15728640 | tf_op jit(solution)/shard_map/add | solution.py:241
  400.6 33.4 %copy.6 = bf16[32,1536,512]{2,1,0:T(8,128)(2,1)} copy(bf16[32,1536,512]{2,1,0:T(8,128)(2,1)} %muon_step.1) | data formatting | bytes 100663296
Async XLA Ops:
  0.6 393.0 %copy-start = (bf16[32,96,512]{2,1,0:T(8,128)(2,1)S(1)}, bf16[32,96,512]{2,1,0:T(8,128)(2,1)}, u32[]{:S(2)}) copy-start(bf16[32,96,512]{2,1,0:T(8,128)(2,1)} %grad_hbm.1) | copy-start | bytes 9437188

commit v2 on v1

--- a/solution.py
+++ b/solution.py
@@ -22,8 +22,9 @@
 BF16 = jnp.bfloat16
 
 
-def hops(quad):
-    return (4, 3) if quad % 2 == 0 else (3, 4)
+RING_HOPS = 3
+SLOTS = 12
+LAG = 6
 
 
 def newton_schulz(x_ref, gram_ref, poly_ref, denom):
@@ -62,7 +63,7 @@
     lax.fori_loop(0, NS_ITERS, iteration, 0)
 
 
-def step_kernel(group, w_hbm, mom_hbm, grad_hbm, out_hbm,
+def step_kernel(group, w_hbm, mom_hbm, grad_hbm, out_hbm, far_up, far_down,
                 mom_v, grad_v, w_v, mom_b, x_v, o_v, new_v, sq_out, sq_in, gram_v, poly_v,
                 in_sem, w_sem, a_send, a_recv, q_send, q_recv, o_send, o_recv,
                 ring_send, ring_recv, pair_send, pair_recv, own_sem):
@@ -163,17 +164,20 @@
             remote(src, dst, pair_send.at[0], pair_recv.at[0], pair).start()
             pltpu.make_async_copy(src, dst, own_sem.at[s]).start()
 
+    def landing(s, q, way, h, src):
+        if h == RING_HOPS and q % 2 == way:
+            return (far_up, far_down)[way].at[pl.ds((s * (QUADS // 2) + q // 2) * quad_mats, quad_mats)]
+        return block(out_hbm, s, q, src)
+
     def relay(s, h):
         for q in range(QUADS):
             for way in range(2):
-                if h > hops(q)[way]:
-                    continue
                 src = lax.rem(chip + (chips - h if way == 0 else h), chips) * CORES + core
-                blk = block(out_hbm, s, q, src)
-                remote(blk, blk, ring_send.at[way], ring_recv.at[way, s, q, h - 1], (up, down)[way]).wait_recv()
-                if h < hops(q)[way]:
-                    remote(blk, blk, ring_send.at[way], ring_recv.at[way, s, q, h], (up, down)[way]).start()
-                remote(blk, blk, pair_send.at[0], pair_recv.at[0], pair).start()
+                got = landing(s, q, way, h, src)
+                remote(got, got, ring_send.at[way], ring_recv.at[way, s, q, h - 1], (up, down)[way]).wait_recv()
+                if h < RING_HOPS:
+                    remote(got, landing(s, q, way, h + 1, src), ring_send.at[way], ring_recv.at[way, s, q, h], (up, down)[way]).start()
+                remote(got, block(out_hbm, s, q, src), pair_send.at[0], pair_recv.at[0], pair).start()
 
     update(0)
     relay(0, 1)
@@ -182,9 +186,7 @@
     relay(1, 1)
     relay(0, 3)
     relay(1, 2)
-    relay(0, 4)
     relay(1, 3)
-    relay(1, 4)
 
     others = pl.ds(0, group - 1)
     for s in range(2):
@@ -194,12 +196,169 @@
         own = new_v.at[pl.ds(s * group, group)]
         pltpu.make_async_copy(own, own, own_sem.at[s]).wait()
     for way in range(2):
-        sent = sum(hops(q)[way] for q in range(QUADS)) * quad_mats * 2
-        full = out_hbm.at[pl.ds(0, sent // group)]
+        full = out_hbm.at[pl.ds(0, RING_HOPS * count // group)]
         pltpu.make_async_copy(full, full, ring_send.at[way]).wait()
-    full = out_hbm.at[pl.ds(0, count // 2)]
+    full = out_hbm.at[pl.ds(0, (2 * RING_HOPS + 1) * count // group)]
     pltpu.make_async_copy(full, full, pair_send.at[0]).wait()
     pltpu.make_async_copy(full, full, pair_recv.at[0]).wait()
+
+
+def assemble_kernel(group, gath, far_up, far_down, mom_hbm, grad_hbm, out_hbm, mom_out,
+                    buf, mom_v, grad_v, in_sem, out_sem, mom_in, mom_done):
+    count, rows, cols = mom_hbm.shape
+    chips = group // CORES
+    quads = 2 * QUADS
+    quad_mats = count // quads
+    me = lax.axis_index("data")
+    chip, core = me // CORES, me % CORES
+    per_chip = CORES * quads
+    total = (2 * RING_HOPS + 1) * per_chip
+    every = total // quads
+
+    def where(i):
+        j, c, g = i // per_chip, (i // quads) % CORES, i % quads
+        src = lax.rem(chip + j + chips - RING_HOPS, chips) * CORES + c
+        return j, c, g, src
+
+    def block(ref, g, src):
+        return ref.at[pl.ds(g * quad_mats, quad_mats), pl.ds(pl.multiple_of(src * rows, 32), rows), :]
+
+    def load(i):
+        j, c, g, src = where(i)
+        slot = i % SLOTS
+        up_far = (j == 0) & (c == core) & (g % 2 == 0)
+        down_far = (j == 2 * RING_HOPS) & (c == core) & (g % 2 == 1)
+        far = pl.ds((g // 2) * quad_mats, quad_mats)
+
+        @pl.when(up_far)
+        def _():
+            pltpu.make_async_copy(far_up.at[far], buf.at[slot], in_sem.at[slot]).start()
+
+        @pl.when(down_far)
+        def _():
+            pltpu.make_async_copy(far_down.at[far], buf.at[slot], in_sem.at[slot]).start()
+
+        @pl.when(jnp.logical_not(up_far | down_far))
+        def _():
+            pltpu.make_async_copy(block(gath, g, src), buf.at[slot], in_sem.at[slot]).start()
+
+    def store(i):
+        _, _, g, src = where(i)
+        slot = i % SLOTS
+        return pltpu.make_async_copy(buf.at[slot], block(out_hbm, g, src), out_sem.at[slot])
+
+    def step(i, carry):
+        slot = i % SLOTS
+
+        @pl.when((i >= SLOTS) & (i < total))
+        def _():
+            store(i - SLOTS).wait()
+
+        @pl.when(i < total)
+        def _():
+            load(i)
+
+        @pl.when(i >= LAG)
+        def _():
+            late = (i - LAG) % SLOTS
+            pltpu.make_async_copy(buf.at[late], buf.at[late], in_sem.at[late]).wait()
+            store(i - LAG).start()
+
+        t = i // every
+        mats = pl.ds(t * quad_mats, quad_mats)
+
+        @pl.when((i % every == 0) & (i < total))
+        def _():
+            pltpu.make_async_copy(mom_hbm.at[mats], mom_v.at[mats], mom_in.at[0, t]).start()
+            pltpu.make_async_copy(grad_hbm.at[mats], grad_v.at[mats], mom_in.at[1, t]).start()
+
+        @pl.when((i % every == every - 1) & (i < total))
+        def _():
+            pltpu.make_async_copy(mom_hbm.at[mats], mom_v.at[mats], mom_in.at[0, t]).wait()
+            pltpu.make_async_copy(grad_hbm.at[mats], grad_v.at[mats], mom_in.at[1, t]).wait()
+
+            def one(m, inner):
+                mom_v[m] = MOMENTUM * mom_v[m] + grad_v[m].astype(F32)
+                return inner
+            lax.fori_loop(t * quad_mats, (t + 1) * quad_mats, one, 0)
+            pltpu.make_async_copy(mom_v.at[mats], mom_out.at[mats], mom_done.at[t]).start()
+        return carry
+
+    lax.fori_loop(0, total + LAG, step, 0)
+
+    def drain(i, carry):
+        store(i).wait()
+        return carry
+    lax.fori_loop(total - SLOTS, total, drain, 0)
+    for t in range(quads):
+        mats = pl.ds(t * quad_mats, quad_mats)
+        pltpu.make_async_copy(mom_v.at[mats], mom_out.at[mats], mom_done.at[t]).wait()
+
+
+def place_kernel(group, other_core, prev, even, odd, out_hbm, buf, in_sem, out_sem):
+    count = prev.shape[0]
+    _, rows, _ = even.shape
+    chips = group // CORES
+    quads = 2 * QUADS
+    quad_mats = count // quads
+    me = lax.axis_index("data")
+    chip, core = me // CORES, me % CORES
+    src = lax.rem(chip + chips // 2, chips) * CORES + (1 - core if other_core else core)
+
+    def load(g):
+        ref = (even, odd)[g % 2]
+        return pltpu.make_async_copy(ref.at[pl.ds((g // 2) * quad_mats, quad_mats)], buf.at[g], in_sem.at[g])
+
+    def store(g):
+        rows_of = pl.ds(pl.multiple_of(src * rows, 32), rows)
+        return pltpu.make_async_copy(buf.at[g], out_hbm.at[pl.ds(g * quad_mats, quad_mats), rows_of, :], out_sem.at[g])
+
+    for g in range(quads):
+        load(g).start()
+    for g in range(quads):
+        load(g).wait()
+        store(g).start()
+    for g in range(quads):
+        store(g).wait()
+
+
+def assemble(group, gath, far_up, far_down, mom_rows, grad_rows):
+    count, rows, cols = mom_rows.shape
+    quads = 2 * QUADS
+    any_spec = pl.BlockSpec(memory_space=pltpu.HBM)
+    dma = pltpu.SemaphoreType.DMA
+    return pl.pallas_call(
+        functools.partial(assemble_kernel, group),
+        out_shape=(jax.ShapeDtypeStruct(gath.shape, BF16), jax.ShapeDtypeStruct((count, rows, cols), F32)),
+        in_specs=[any_spec] * 5,
+        out_specs=(any_spec, any_spec),
+        scratch_shapes=[
+            pltpu.VMEM((SLOTS, count // quads, rows, cols), BF16),
+            pltpu.VMEM((count, rows, cols), F32),
+            pltpu.VMEM((count, rows, cols), BF16),
+            dma((SLOTS,)), dma((SLOTS,)), dma((2, quads)), dma((quads,)),
+        ],
+        compiler_params=pltpu.CompilerParams(vmem_limit_bytes=60 * 1024 * 1024),
+        cost_estimate=pl.CostEstimate(flops=200_000_000, bytes_accessed=4 * gath.size, transcendentals=0),
+        name="assemble",
+    )(gath, far_up, far_down, mom_rows, grad_rows)
+
+
+def place(group, other_core, prev, even, odd):
+    count = prev.shape[0]
+    quads = 2 * QUADS
+    any_spec = pl.BlockSpec(memory_space=pltpu.HBM)
+    dma = pltpu.SemaphoreType.DMA
+    return pl.pallas_call(
+        functools.partial(place_kernel, group, other_core),
+        out_shape=jax.ShapeDtypeStruct(prev.shape, BF16),
+        in_specs=[any_spec] * 3,
+        out_specs=any_spec,
+        input_output_aliases={0: 0},
+        scratch_shapes=[pltpu.VMEM((quads, count // quads) + even.shape[1:], BF16), dma((quads,)), dma((quads,))],
+        cost_estimate=pl.CostEstimate(flops=20_000_000, bytes_accessed=8 * even.size, transcendentals=0),
+        name="place_other" if other_core else "place_own",
+    )(prev, even, odd)
 
 
 def run_step(group, w_rows, mom_rows, grad_rows):
@@ -208,9 +367,13 @@
     dma = pltpu.SemaphoreType.DMA
     return pl.pallas_call(
         functools.partial(step_kernel, group),
-        out_shape=jax.ShapeDtypeStruct((count, rows * group, cols), BF16),
+        out_shape=(
+            jax.ShapeDtypeStruct((count, rows * group, cols), BF16),
+            jax.ShapeDtypeStruct((count // 2, rows, cols), BF16),
+            jax.ShapeDtypeStruct((count // 2, rows, cols), BF16),
+        ),
         in_specs=[any_spec] * 3,
-        out_specs=any_spec,
+        out_specs=(any_spec,) * 3,
         scratch_shapes=[
             pltpu.VMEM((count, rows, cols), F32),
             pltpu.VMEM((count, rows, cols), BF16),
@@ -225,7 +388,7 @@
             pltpu.VMEM((cols, cols), BF16),
             dma((2, count)), dma((2,)),
             dma((2,)), dma((2,)), dma((2,)), dma((2,)), dma((2,)), dma((2,)),
-            dma((2,)), dma((2, 2, QUADS, 4)), dma((1,)), dma((1,)), dma((2,)),
+            dma((2,)), dma((2, 2, QUADS, RING_HOPS)), dma((1,)), dma((1,)), dma((2,)),
         ],
         compiler_params=pltpu.CompilerParams(collective_id=0, has_side_effects=True, vmem_limit_bytes=60 * 1024 * 1024),
         name="muon_step",
@@ -238,8 +401,16 @@
     full_spec = P("stage", None, None)
 
     def local_step(w_rows, mom_rows, grad_rows):
-        mom_new = MOMENTUM * mom_rows + grad_rows.astype(F32)
-        params = run_step(group, w_rows, mom_rows, grad_rows)
+        gath, far_up, far_down = run_step(group, w_rows, mom_rows, grad_rows)
+        last_up = lax.ppermute(far_up, "data", [(d, (d + CORES) % group) for d in range(group)])
+        last_down = lax.ppermute(far_down, "data", [(d, (d - CORES) % group) for d in range(group)])
+        params, mom_new = assemble(group, gath, far_up, far_down, mom_rows, grad_rows)
+        last_up, last_down, params = lax.optimization_barrier((last_up, last_down, params))
+        pairs = [(d, d ^ 1) for d in range(group)]
+        pair_up = lax.ppermute(last_up, "data", pairs)
+        pair_down = lax.ppermute(last_down, "data", pairs)
+        params = place(group, False, params, last_up, last_down)
+        params = place(group, True, params, pair_up, pair_down)
         return params, mom_new
 
     return jax.shard_map(local_step, mesh=mesh, in_specs=(row_spec, row_spec, row_spec), out_specs=(full_spec, row_spec), check_vma=False)

time: 434 us -> 407 us (0.938)
  local copies, waits for them, and re-layouts: 33.5 us -> 0.62 us
  Pallas kernels: 393 us -> 400 us
  other arithmetic: 6.9 us -> 0 us
    unnamed x3 -> x4, local copies, waits for them, and re-layouts: 33.5 us -> 0.62 us
    add x1 -> x0, other arithmetic: 6.9 us -> none  [local_step(): mom_new = MOMENTUM * mom_rows + grad_rows.astype(F32)]
    pallas_call x1 -> x4, Pallas kernels: 393 us -> 400 us  [the longest x1 359 us: run_step(): pl.pallas_call(functools.partial(step_kernel, group), out_shape=(jax.Shap...]
  transfers between devices with their start and end apart: 0 -> 4, of which waited for: 0 -> 1; matrix products, arithmetic and copies ran while one was open for 0% -> 0% of each run, Pallas kernels for 0% -> 9%
where the time goes in v2:
time: 407 us; the launch traced here: 406 us
  Pallas kernels  400 us (98%)
    pallas_call x1, Pallas kernels, run_step(): pl.pallas_call(functools.partial(step_kernel, group), out_shape=(jax.Shap...  359 us
    pallas_call x1, Pallas kernels, assemble(): pl.pallas_call(functools.partial(assemble_kernel, group), out_shape=(jax....  34.9 us
  transfers between devices with their start and end apart: 4, of which 1 were waited for; matrix products, arithmetic and copies ran while one was open for 0% of the time, Pallas kernels for 9%

profile of v2, /device:TPU:21, one launch (start us, length us, event | category | flops | bytes accessed | tf_op | source)
XLA Modules:
  0.0 406.4 jit_solution(10579991994168799999)
XLA Ops:
  0.6 359.2 %muon_step.1 = (bf16[32,1536,512]{2,1,0:T(8,128)(2,1)}, bf16[16,96,512]{2,1,0:T(8,128)(2,1)}, bf16[16,96,512]{2,1,0:T(8,128)(2,1)}) custom-call(f32[32,96,512]{2,1,0:T(8,128)} %w_hbm.1, f32[32,96,512]{2,1,0:T(8,128)} %mom_hbm.3, bf16[32,96,512]{2,1,0:T(8,128)(2,1)} %grad_hbm.3), custom_call_target="tpu_custom_call" | custom-call | tf_op jit(solution)/shard_map/muon_step/pallas_call | solution.py:368
  359.8 0.1 collective-permute-start
  359.9 2.7 collective-permute-start.1
  362.6 34.9 %assemble.1 = (bf16[32,1536,512]{2,1,0:T(8,128)(2,1)}, f32[32,96,512]{2,1,0:T(8,128)}) custom-call(bf16[32,1536,512]{2,1,0:T(8,128)(2,1)} %get-tuple-element.12.gath, bf16[16,96,512]{2,1,0:T(8,128)(2,1)} %get-tuple-element.10.far_up, bf16[16,96,512]{2,1,0:T(8,128)(2,1)} %get-tuple-element.11.far_down, f32[32,96,512]{2,1,0:T(8,128)} %mom_hbm.3, ...), custom_call_target="tpu_custom_call" | custom-call | flops 200000000 | bytes 100663296 | tf_op jit(solution)/shard_map/assemble/pallas_call | solution.py:330
  397.4 0.0 collective-permute-done.even
  397.4 0.0 copy-start
  397.5 0.0 collective-permute-done.1.odd
  397.5 0.0 copy-start.1
  397.5 0.9 collective-permute-start.2
  398.3 0.1 collective-permute-start.3
  398.5 0.1 copy-done
  398.6 0.5 copy-done.1
  399.1 2.8 place_own.1.prev
  401.9 0.0 collective-permute-done.2.even
  401.9 1.7 collective-permute-done.3.odd
  403.6 2.8 place_other.1
Async XLA Ops:
  359.8 37.6 %collective-permute-start = (bf16[16,96,512]{2,1,0:T(8,128)(2,1)}, bf16[16,96,512]{2,1,0:T(8,128)(2,1)S(1)}, u32[]{:S(2)}, u32[]{:S(2)}) collective-permute-start(bf16[16,96,512]{2,1,0:T(8,128)(2,1)} %get-tuple-element.10.far_up), channel_id=1, source_target_pairs={{0,2},{1,3},{2,4},{3,5},{4,6},{5,7},{6,8},{7,9},{8,10},{9,11},{10,... | collective-permute-start | bytes 4718600 | tf_op jit(solution)/shard_map/ppermute | solution.py:405
  359.9 37.5 %collective-permute-start.1 = (bf16[16,96,512]{2,1,0:T(8,128)(2,1)}, bf16[16,96,512]{2,1,0:T(8,128)(2,1)S(1)}, u32[]{:S(2)}, u32[]{:S(2)}) collective-permute-start(bf16[16,96,512]{2,1,0:T(8,128)(2,1)} %get-tuple-element.11.far_down), channel_id=1, source_target_pairs={{0,14},{1,15},{2,0},{3,1},{4,2},{5,3},{6,4},{7,5},{8,6},{9,7},{10,... | collective-permute-start | bytes 4718600 | tf_op jit(solution)/shard_map/ppermute | solution.py:406
  397.4 1.1 copy-start
  397.5 1.6 copy-start.1
  397.5 4.4 %collective-permute-start.2 = (bf16[16,96,512]{2,1,0:T(8,128)(2,1)S(1)}, bf16[16,96,512]{2,1,0:T(8,128)(2,1)}, u32[]{:S(2)}, u32[]{:S(2)}) collective-permute-start(bf16[16,96,512]{2,1,0:T(8,128)(2,1)S(1)} %collective-permute-done.even), channel_id=1, source_target_pairs={{0,1},{1,0},{2,3},{3,2},{4,5},{5,4},{6,7},{7,6},{8,9},{9,8},{10,11... | collective-permute-start | bytes 4718600 | tf_op jit(solution)/shard_map/ppermute | solution.py:410
  398.3 5.3 %collective-permute-start.3 = (bf16[16,96,512]{2,1,0:T(8,128)(2,1)S(1)}, bf16[16,96,512]{2,1,0:T(8,128)(2,1)}, u32[]{:S(2)}, u32[]{:S(2)}) collective-permute-start(bf16[16,96,512]{2,1,0:T(8,128)(2,1)S(1)} %collective-permute-done.1.odd), channel_id=1, source_target_pairs={{0,1},{1,0},{2,3},{3,2},{4,5},{5,4},{6,7},{7,6},{8,9},{9,8},{10,11... | collective-permute-start | bytes 4718600 | tf_op jit(solution)/shard_map/ppermute | solution.py:411
